TPU v7x, 32 devices: a whole 2x2x4 slice. The times are simulated.
32 devices in a mesh: blk: 4 (over z), tp: 8 (over y, x, core).
Axes of the slice: x: 2, y: 2, z: 4, core: 2. Of those that a mesh axis runs over, the one named last changes fastest.
Arguments:
- input_pool: bfloat16 [4096, 1792], P(None, 'tp'), may hold values from -6 to 6
- teacher_pool: bfloat16 [4096, 1792], P(None, 'tp'), may hold values from -6 to 6
- gate_weight: bfloat16 [1792, 9472], P(None, 'tp'), may hold values from -0.125 to 0.125
- up_weight: bfloat16 [1792, 9472], P(None, 'tp'), may hold values from -0.125 to 0.125
- params: float32 [4, 9472, 1792], P('blk', 'tp'), may hold values from -6 to 6
- batch_ids: int32 [4, 1024], replicated, may hold values from 0 to 4095
- cycle_order: int32 [4], replicated, may hold values from 0 to 3, each once
- edge_weight: float32 [4], replicated, may hold values from 0.1 to 0.45
Outputs:
- updated: float32 [4, 9472, 1792], P('blk', 'tp')
Inputs may be any that keep to these rules, and one draw needn't show every extreme that they name: `cycle_order`: the 4 cycle positions name 4 different agents.
All inputs are finite; a program needn't handle non-finite values.
Results may differ from a plain program's by a relative error of at most 0.0061.
Values may be sent and summed in bfloat16 or wider, within the bound.
A program may use at most 128 MiB of HBM per device.

v0:
```python
import jax
import jax.numpy as jnp
from jax import lax
from jax.sharding import PartitionSpec as P


def shifted(array, axis, by):
    count = lax.axis_size(axis)
    return lax.ppermute(array, axis, [(i, (i + by) % count) for i in range(count)])


def body(
    input_pool, teacher_pool, gate_weight, up_weight, params, batch_ids, cycle_order, edge_weight
):
    step_rate = 2.0
    groups = lax.axis_size("tp")
    place = lax.axis_index("blk")
    agents = cycle_order.shape[0]
    slots = jnp.arange(agents, dtype=jnp.int32)
    here = slots == place
    before = slots == (place + agents - 1) % agents
    agent = jnp.sum(jnp.where(here, cycle_order, 0))
    weight_next = jnp.sum(jnp.where(here, edge_weight, 0.0))
    weight_prev = jnp.sum(jnp.where(before, edge_weight, 0.0))
    weight_self = 1.0 - weight_next - weight_prev
    batch = lax.dynamic_slice_in_dim(batch_ids, agent, 1, 0)[0]
    inputs_local = jnp.take(input_pool, batch, axis=0)
    teacher_local = jnp.take(teacher_pool, batch, axis=0)
    hidden_dev = gate_weight.shape[1]
    scale = float(hidden_dev * groups) ** (-0.5)
    rows = lax.all_gather(inputs_local, "tp", axis=1, tiled=True)
    gate = jnp.dot(rows, gate_weight, preferred_element_type=jnp.float32)
    up = jnp.dot(rows, up_weight, preferred_element_type=jnp.float32)
    teacher = lax.all_gather(teacher_local, "tp", axis=1, tiled=True)
    gate, up, teacher_full = (gate, up, teacher)
    hidden = (jax.nn.silu(gate) * up).astype(jnp.bfloat16)

    def gradient(weights):
        weights_half = weights.astype(jnp.bfloat16)
        partial_out = scale * jnp.dot(hidden, weights_half, preferred_element_type=jnp.float32)
        output = lax.psum(partial_out, "tp")
        resid = (output - teacher_full.astype(jnp.float32)).astype(jnp.bfloat16)
        return scale * lax.dot_general(
            hidden, resid, (((0,), (0,)), ((), ())), preferred_element_type=jnp.float32
        )

    start_field = params[0]
    grad_first = gradient(start_field)

    def mix_two(field):
        lower = shifted(field, "blk", 1)
        upper = shifted(field, "blk", -1)
        return weight_self * field + weight_next * upper + weight_prev * lower

    moved = mix_two(start_field) - step_rate * grad_first
    combined = moved - step_rate * grad_first
    grad_second = gradient(moved)
    result = mix_two(combined) - step_rate * (grad_second - grad_first)
    return result[None]


def solution(mesh):
    placed = (
        P(None, "tp"),
        P(None, "tp"),
        P(None, "tp"),
        P(None, "tp"),
        P("blk", "tp", None),
        P(),
        P(),
        P(),
    )
    return jax.shard_map(
        body, mesh=mesh, in_specs=placed, out_specs=P("blk", "tp", None), check_vma=False
    )
```

profile of v0, /device:TPU:0, one launch (start us, length us, event | category | flops | bytes accessed | tf_op | source)
XLA Modules:
  0.0 809.0 jit_solution(17603481513020024617)
XLA Ops:
  6.5 1.3 fusion.11
  9.8 4.0 copy.11
  13.8 3.2 copy.13
  17.0 5.3 gather_fusion
  22.4 3.9 gather_fusion.1
  26.5 1.0 copy.12
  28.6 5.1 collective-permute-start
  33.7 31.0 %all-gather.3.cloned.1.call-done = bf16[1024,1792]{0,1:T(8,128)(2,1)} async-done(((bf16[1024,224]{0,1:T(8,128)(2,1)}), bf16[1024,1792]{0,1:T(8,128)(2,1)}) %all-gather.3.cloned.1.call-update) | async-done | bytes 3670032 | tf_op jit(solution)/shard_map/all_gather | solution.py:31
  64.8 7.6 fusion.17
  72.4 8.0 multiply_convert_fusion
  80.4 1.5 copy-done.2
  81.8 7.2 convolution_multiply_fusion.2
  91.6 9.5 %all-gather.5.cloned.1.call-done = bf16[1024,1792]{0,1:T(8,128)(2,1)} async-done(((bf16[1024,224]{0,1:T(8,128)(2,1)}), bf16[1024,1792]{0,1:T(8,128)(2,1)}) %all-gather.5.cloned.1.call-update) | async-done | bytes 3670032 | tf_op jit(solution)/shard_map/all_gather | solution.py:34
  101.1 115.9 %collective-permute-done = f32[1184,1792]{1,0:T(8,128)} collective-permute-done((f32[1184,1792]{1,0:T(8,128)}, f32[1184,1792]{1,0:T(8,128)}, u32[]{:S(2)}, u32[]{:S(2)}) %collective-permute-start) | collective-permute-done | bytes 8486944 | tf_op jit(solution)/shard_map/ppermute | solution.py:9
  217.0 181.6 %collective-permute-done.1 = f32[1184,1792]{1,0:T(8,128)} collective-permute-done((f32[1184,1792]{1,0:T(8,128)}, f32[1184,1792]{1,0:T(8,128)}, u32[]{:S(2)}, u32[]{:S(2)}) %collective-permute-start.1) | collective-permute-done | bytes 8486944 | tf_op jit(solution)/shard_map/ppermute | solution.py:9
  398.6 22.6 %multiply_subtract_fusion = (f32[1184,1792]{1,0:T(8,128)}, bf16[1184,1792]{1,0:T(8,128)(2,1)S(1)}, f32[1184,1792]{1,0:T(8,128)}) fusion(f32[1184,1792]{1,0:T(8,128)} %collective-permute-done.1, f32[]{:T(128)} %get-tuple-element.7, f32[1184,1792]{1,0:T(8,128)} %collective-permute-done, f32[]{:T(128)} %get-tuple-element.6, f32[1,1184,1792]{2,1,0:T(8,128)} %param.14, ...), kind=kOutput, calls=%fused_computation.9 | convolution fusion | flops 4369899520 | bytes 60112908 | tf_op jit(solution)/shard_map/dot_general | solution.py:43
  421.2 1.6 collective-permute-start.3
  422.9 2.2 collective-permute-start.2
  425.1 8.7 %convolution_multiply_fusion.1 = f32[1024,1792]{0,1:T(8,128)} fusion(bf16[1024,1184]{0,1:T(8,128)(2,1)} %copy-done.2, bf16[1184,1792]{1,0:T(8,128)(2,1)S(1)} %get-tuple-element.9), kind=kOutput, calls=%fused_computation.13 | convolution fusion | flops 4347133952 | bytes 14008320 | tf_op jit(solution)/shard_map/dot_general | solution.py:40
  433.8 113.8 %all-reduce.5.cloned.1.call-done = f32[1024,1792]{0,1:T(8,128)} async-done(((f32[1024,1792]{0,1:T(8,128)}), f32[1024,1792]{0,1:T(8,128)}) %all-reduce.5.cloned.1.call-update) | async-done | bytes 7340048 | tf_op jit(solution)/shard_map/psum | solution.py:41
  547.6 12.8 %fusion.1 = f32[1184,1792]{1,0:T(8,128)} fusion(bf16[1024,1184]{0,1:T(8,128)(2,1)S(1)} %copy-done.3, f32[1184,1792]{1,0:T(8,128)} %get-tuple-element.12, f32[1024,1792]{0,1:T(8,128)} %all-reduce.5.cloned.1.call-done, bf16[1024,1792]{0,1:T(8,128)(2,1)} %all-gather.5.cloned.1.call-done), kind=kOutput, calls=%fused_computation.6 | convolution fusion | flops 4359290880 | bytes 30408704 | tf_op jit(solution)/shard_map/dot_general | solution.py:43
  560.5 48.3 %collective-permute-done.3 = f32[1184,1792]{1,0:T(8,128)} collective-permute-done((f32[1184,1792]{1,0:T(8,128)}, f32[1184,1792]{1,0:T(8,128)}, u32[]{:S(2)}, u32[]{:S(2)}) %collective-permute-start.3) | collective-permute-done | bytes 8486944 | tf_op jit(solution)/shard_map/ppermute | solution.py:9
  608.8 179.5 %collective-permute-done.2 = f32[1184,1792]{1,0:T(8,128)} collective-permute-done((f32[1184,1792]{1,0:T(8,128)}, f32[1184,1792]{1,0:T(8,128)}, u32[]{:S(2)}, u32[]{:S(2)}) %collective-permute-start.2) | collective-permute-done | bytes 8486944 | tf_op jit(solution)/shard_map/ppermute | solution.py:9
  788.3 14.1 %subtract_bitcast_fusion = f32[1,1184,1792]{2,1,0:T(8,128)} fusion(f32[1184,1792]{1,0:T(8,128)} %fusion.1, f32[1184,1792]{1,0:T(8,128)} %collective-permute-done.3, f32[1184,1792]{1,0:T(8,128)} %collective-permute-done.2, f32[1184,1792]{1,0:T(8,128)S(1)} %bitcast.29, f32[]{:T(128)} %get-tuple-element.7, f32[]{:T(128)} %get-tuple-element.6, f32[]{:T(128)S(6)} %sub.29), kind=kLoop, calls=%fused_computation.7 | loop fusion | flops 12730368 | bytes 42434572 | tf_op jit(solution)/shard_map/broadcast_in_dim | solution.py:59
  (41 shorter events, 2.7 us)
Async XLA Ops:
  6.5 3.3 copy-start
  6.5 58.2 %all-gather.3.cloned.1.call-start = ((), (), s32[]{:S(2)}) async-start(), calls=%async_computation | async-start | bytes 4128768 | tf_op jit(solution)/shard_map/all_gather | solution.py:31
  27.5 73.6 %all-gather.5.cloned.1.call-start = ((), (), s32[]{:S(2)}) async-start(), calls=%async_computation.2 | async-start | bytes 4128768 | tf_op jit(solution)/shard_map/all_gather | solution.py:34
  28.5 370.1 %all-reduce.3.cloned.1.call-start = ((), (), s32[]{:S(2)}) async-start(), calls=%async_computation.1 | async-start | bytes 14680064 | tf_op jit(solution)/shard_map/psum | solution.py:41
  28.6 188.4 %collective-permute-start = (f32[1184,1792]{1,0:T(8,128)}, f32[1184,1792]{1,0:T(8,128)}, u32[]{:S(2)}, u32[]{:S(2)}) collective-permute-start(f32[1184,1792]{1,0:T(8,128)} %bitcast.30), channel_id=1, source_target_pairs={{0,24},{8,0},{16,8},{24,16},{1,25},{9,1},{17,9},{25,17},{2,26},{10... | collective-permute-start | bytes 25460744 | tf_op jit(solution)/shard_map/ppermute | solution.py:9
  33.7 364.9 %collective-permute-start.1 = (f32[1184,1792]{1,0:T(8,128)}, f32[1184,1792]{1,0:T(8,128)}, u32[]{:S(2)}, u32[]{:S(2)}) collective-permute-start(f32[1184,1792]{1,0:T(8,128)} %bitcast.31), channel_id=1, source_target_pairs={{0,8},{8,16},{16,24},{24,0},{1,9},{9,17},{17,25},{25,1},{2,10},{10... | collective-permute-start | bytes 25460744 | tf_op jit(solution)/shard_map/ppermute | solution.py:9
  64.8 7.6 copy-start.5
  64.8 17.1 %slice-start.3 = ((s8[8486912]{0:T(1024)(128)(4,1)}), s8[4194304]{0:T(1024)(128)(4,1)S(1)}, s32[]{:S(2)}) async-start(s8[8486912]{0:T(1024)(128)(4,1)} %bitcast.32), calls=%async_computation.7 | async-start | bytes 8388608
  64.8 17.1 %slice-start.4 = ((s8[8486912]{0:T(1024)(128)(4,1)}), s8[4194304]{0:T(1024)(128)(4,1)S(1)}, s32[]{:S(2)}) async-start(s8[8486912]{0:T(1024)(128)(4,1)} %bitcast.32), calls=%async_computation.8 | async-start | bytes 8388608
  72.4 9.5 %slice-start.5 = ((s8[8486912]{0:T(1024)(128)(4,1)}), s8[98304]{0:T(1024)(128)(4,1)S(1)}, s32[]{:S(2)}) async-start(s8[8486912]{0:T(1024)(128)(4,1)} %bitcast.32), calls=%async_computation.9 | async-start | bytes 196608
  80.4 1.5 copy-start.2
  89.1 0.7 copy-start.4
  89.1 458.6 %all-reduce.5.cloned.1.call-start = ((), (), s32[]{:S(2)}) async-start(), calls=%async_computation.3 | async-start | bytes 14680064 | tf_op jit(solution)/shard_map/psum | solution.py:41
  421.2 187.5 %collective-permute-start.3 = (f32[1184,1792]{1,0:T(8,128)}, f32[1184,1792]{1,0:T(8,128)}, u32[]{:S(2)}, u32[]{:S(2)}) collective-permute-start(f32[1184,1792]{1,0:T(8,128)} %get-tuple-element.8), channel_id=1, source_target_pairs={{0,8},{8,16},{16,24},{24,0},{1,9},{9,17},{17,25},{25,1},{2,10},{10... | collective-permute-start | bytes 25460744 | tf_op jit(solution)/shard_map/ppermute | solution.py:9
  422.9 365.4 %collective-permute-start.2 = (f32[1184,1792]{1,0:T(8,128)}, f32[1184,1792]{1,0:T(8,128)}, u32[]{:S(2)}, u32[]{:S(2)}) collective-permute-start(f32[1184,1792]{1,0:T(8,128)} %get-tuple-element.8), channel_id=1, source_target_pairs={{0,24},{8,0},{16,8},{24,16},{1,25},{9,1},{17,9},{25,17},{2,26},{10... | collective-permute-start | bytes 25460744 | tf_op jit(solution)/shard_map/ppermute | solution.py:9
  433.8 113.8 %copy-start.3 = (bf16[1024,1184]{0,1:T(8,128)(2,1)S(1)}, bf16[1024,1184]{0,1:T(8,128)(2,1)}, u32[]{:S(2)}) copy-start(bf16[1024,1184]{0,1:T(8,128)(2,1)} %copy-done.2) | copy-start | bytes 7274500
  433.8 354.5 %slice-start = ((s8[8486912]{0:T(1024)(128)(4,1)}), s8[98304]{0:T(1024)(128)(4,1)S(1)}, s32[]{:S(2)}) async-start(s8[8486912]{0:T(1024)(128)(4,1)} %bitcast.28), calls=%async_computation.4 | async-start | bytes 196608
  547.6 240.6 %slice-start.1 = ((s8[8486912]{0:T(1024)(128)(4,1)}), s8[4194304]{0:T(1024)(128)(4,1)S(1)}, s32[]{:S(2)}) async-start(s8[8486912]{0:T(1024)(128)(4,1)} %bitcast.28), calls=%async_computation.5 | async-start | bytes 8388608
  547.6 240.6 %slice-start.2 = ((s8[8486912]{0:T(1024)(128)(4,1)}), s8[4194304]{0:T(1024)(128)(4,1)S(1)}, s32[]{:S(2)}) async-start(s8[8486912]{0:T(1024)(128)(4,1)} %bitcast.28), calls=%async_computation.6 | async-start | bytes 8388608
  788.3 14.2 %copy-start.1 = (s32[4,1024]{1,0:T(4,128)S(1)}, s32[4,1024]{1,0:T(4,128)}, u32[]{:S(2)}) copy-start(s32[4,1024]{1,0:T(4,128)} %param.15) | copy-start | bytes 49156
Sparse Core Ops, SparseCore 0:
  27.6 37.0 all-gather.2
  66.7 34.3 all-gather.4
  104.4 115.4 all-reduce.2
  433.9 113.6 all-reduce.4
where the time goes:
time: 809 us
  waiting for transfers between devices  680 us (84%)
  matrix products  66.9 us (8%)
  local copies, waits for them, and re-layouts  20.5 us (3%)
  between operations  16.4 us (2%)
  other arithmetic  16.3 us (2%)
  starting transfers between devices  9.08 us (1%)
    ppermute x4, waiting for transfers between devices, shifted(): lax.ppermute(array, axis, [(i, (i + by) % count) for i in range(count)])  525 us
    psum x2, waiting for transfers between devices, gradient(): output = lax.psum(partial_out, 'tp')  114 us
    dot_general x2, matrix products, gradient(): lax.dot_general(hidden, resid, (((0,), (0,)), ((), ())), preferred_elemen...  35.4 us
    all_gather x1, waiting for transfers between devices, body(): rows = lax.all_gather(inputs_local, 'tp', axis=1, tiled=True)  31 us
  transfers between devices with their start and end apart: 8, of which 7 were waited for; matrix products, arithmetic and copies ran while one was open for 6% of the time, Pallas kernels for 0%

commit v1 on v0

--- a/solution.py
+++ b/solution.py
@@ -38,7 +38,7 @@
     def gradient(weights):
         weights_half = weights.astype(jnp.bfloat16)
         partial_out = scale * jnp.dot(hidden, weights_half, preferred_element_type=jnp.float32)
-        output = lax.psum(partial_out, "tp")
+        output = lax.all_gather(partial_out, "tp").sum(axis=0)
         resid = (output - teacher_full.astype(jnp.float32)).astype(jnp.bfloat16)
         return scale * lax.dot_general(
             hidden, resid, (((0,), (0,)), ((), ())), preferred_element_type=jnp.float32

time: 809 us -> 875 us (1.082)
  other arithmetic: 16.3 us -> 60.4 us
  waiting for transfers between devices: 680 us -> 703 us
    all_gather x0 -> x2, waiting for transfers between devices: none -> 525 us  [gradient(): output = lax.all_gather(partial_out, 'tp').sum(axis=0)]
    ppermute x4, waiting for transfers between devices: 525 us -> 133 us  [shifted(): lax.ppermute(array, axis, [(i, (i + by) % count) for i in range(count)])]
    psum x2 -> x0, waiting for transfers between devices: 114 us -> none  [gradient(): output = lax.psum(partial_out, 'tp')]
    reduce_sum x0 -> x2, other arithmetic: none -> 44 us  [gradient(): output = lax.all_gather(partial_out, 'tp').sum(axis=0)]
  transfers between devices with their start and end apart: 8 -> 8, of which waited for: 7 -> 6; matrix products, arithmetic and copies ran while one was open for 6% -> 10% of each run, Pallas kernels for 0% -> 0%
where the time goes in v1:
time: 875 us; the launch traced here: 874 us
  waiting for transfers between devices  703 us (80%)
  matrix products  63 us (7%)
  other arithmetic  60.4 us (7%)
  local copies, waits for them, and re-layouts  24.3 us (3%)
  between operations  16.5 us (2%)
    all_gather x2, waiting for transfers between devices, gradient(): output = lax.all_gather(partial_out, 'tp').sum(axis=0)  525 us
    ppermute x4, waiting for transfers between devices, shifted(): lax.ppermute(array, axis, [(i, (i + by) % count) for i in range(count)])  133 us
    reduce_sum x2, other arithmetic, gradient(): output = lax.all_gather(partial_out, 'tp').sum(axis=0)  44 us
    all_gather x1, waiting for transfers between devices, body(): rows = lax.all_gather(inputs_local, 'tp', axis=1, tiled=True)  36.2 us
    dot_general x2, matrix products, gradient(): lax.dot_general(hidden, resid, (((0,), (0,)), ((), ())), preferred_elemen...  30.9 us
  transfers between devices with their start and end apart: 8, of which 6 were waited for; matrix products, arithmetic and copies ran while one was open for 10% of the time, Pallas kernels for 0%

profile of v1, /device:TPU:0, one launch (start us, length us, event | category | flops | bytes accessed | tf_op | source)
XLA Modules:
  0.0 874.3 jit_solution(18031532245252376757)
XLA Ops:
  6.5 1.3 fusion.11
  9.8 4.0 copy.15
  13.8 3.2 copy.17
  17.0 5.3 gather_fusion
  22.4 3.9 gather_fusion.1
  28.6 36.2 %all-gather.7.cloned.1.call-done = bf16[1024,1792]{0,1:T(8,128)(2,1)} async-done(((bf16[1024,224]{0,1:T(8,128)(2,1)}), bf16[1024,1792]{0,1:T(8,128)(2,1)}) %all-gather.7.cloned.1.call-update) | async-done | bytes 3670032 | tf_op jit(solution)/shard_map/all_gather | solution.py:31
  64.8 7.6 fusion.17
  72.4 8.0 multiply_convert_fusion
  80.4 7.3 convolution_multiply_fusion.2
  87.8 3.4 collective-permute-start
  93.1 7.9 all-gather.9.cloned.1.call-done
  101.1 5.9 copy.19
  107.0 263.3 %all-gather.11.cloned.1.call-done = f32[8192,1792]{1,0:T(8,128)} async-done(((f32[1024,1792]{1,0:T(8,128)}), f32[8192,1792]{1,0:T(8,128)}) %all-gather.11.cloned.1.call-update) | async-done | bytes 58720272 | tf_op jit(solution)/shard_map/all_gather | solution.py:41
  370.3 22.0 %reduce_sum.48 = f32[1024,1792]{1,0:T(8,128)} reduce(f32[8,1024,1792]{2,1,0:T(8,128)} %bitcast.30, f32[]{:T(128)} %constant.38.clone.1), dimensions={0}, to_apply=%region_3.5 | reduce | flops 12845056 | bytes 66060292 | tf_op jit(solution)/shard_map/reduce_sum | solution.py:41
  392.3 64.3 %collective-permute-done.1 = f32[1184,1792]{1,0:T(8,128)} collective-permute-done((f32[1184,1792]{1,0:T(8,128)}, f32[1184,1792]{1,0:T(8,128)}, u32[]{:S(2)}, u32[]{:S(2)}) %collective-permute-start.1) | collective-permute-done | bytes 8486944 | tf_op jit(solution)/shard_map/ppermute | solution.py:9
  456.6 20.4 %multiply_subtract_fusion = (f32[1184,1792]{1,0:T(8,128)}, bf16[1184,1792]{1,0:T(8,128)(2,1)}, f32[1184,1792]{1,0:T(8,128)}) fusion(f32[1184,1792]{1,0:T(8,128)} %collective-permute-done.1, f32[]{:T(128)} %get-tuple-element.7, f32[1184,1792]{1,0:T(8,128)} %collective-permute-done, f32[]{:T(128)} %get-tuple-element.6, f32[1,1184,1792]{2,1,0:T(8,128)} %param.14, ...), kind=kOutput, calls=%fused_computation.9 | convolution fusion | flops 4369899520 | bytes 60112908 | tf_op jit(solution)/shard_map/dot_general | solution.py:43
  476.9 9.2 %convolution_multiply_fusion.1 = f32[1024,1792]{1,0:T(8,128)} fusion(bf16[1024,1184]{0,1:T(8,128)(2,1)S(1)} %multiply_convert_fusion, bf16[1184,1792]{1,0:T(8,128)(2,1)} %get-tuple-element.9), kind=kOutput, calls=%fused_computation.13 | convolution fusion | flops 4347133952 | bytes 14008320 | tf_op jit(solution)/shard_map/dot_general | solution.py:40
  486.2 1.6 collective-permute-start.3
  487.7 2.3 collective-permute-start.2
  490.0 261.9 %all-gather.13.cloned.1.call-done = f32[8192,1792]{1,0:T(8,128)} async-done(((f32[1024,1792]{1,0:T(8,128)}), f32[8192,1792]{1,0:T(8,128)}) %all-gather.13.cloned.1.call-update) | async-done | bytes 58720272 | tf_op jit(solution)/shard_map/all_gather | solution.py:41
  752.0 22.0 %reduce_sum.49 = f32[1024,1792]{1,0:T(8,128)} reduce(f32[8,1024,1792]{2,1,0:T(8,128)} %bitcast.31, f32[]{:T(128)} %constant.38.clone.1), dimensions={0}, to_apply=%region_4.6 | reduce | flops 12845056 | bytes 66060292 | tf_op jit(solution)/shard_map/reduce_sum | solution.py:41
  774.0 10.6 %fusion.1 = f32[1184,1792]{1,0:T(8,128)S(1)} fusion(bf16[1024,1184]{0,1:T(8,128)(2,1)S(1)} %multiply_convert_fusion, f32[1184,1792]{1,0:T(8,128)} %get-tuple-element.12, f32[1024,1792]{1,0:T(8,128)} %reduce_sum.49, bf16[1024,1792]{1,0:T(8,128)(2,1)} %copy.19), kind=kOutput, calls=%fused_computation.6 | convolution fusion | flops 4359290880 | bytes 30408704 | tf_op jit(solution)/shard_map/dot_general | solution.py:43
  784.5 69.0 %collective-permute-done.2 = f32[1184,1792]{1,0:T(8,128)} collective-permute-done((f32[1184,1792]{1,0:T(8,128)}, f32[1184,1792]{1,0:T(8,128)}, u32[]{:S(2)}, u32[]{:S(2)}) %collective-permute-start.2) | collective-permute-done | bytes 8486944 | tf_op jit(solution)/shard_map/ppermute | solution.py:9
  853.5 14.3 %subtract_bitcast_fusion = f32[1,1184,1792]{2,1,0:T(8,128)} fusion(f32[1184,1792]{1,0:T(8,128)S(1)} %fusion.1, f32[1184,1792]{1,0:T(8,128)} %collective-permute-done.3, f32[1184,1792]{1,0:T(8,128)} %collective-permute-done.2, f32[1184,1792]{1,0:T(8,128)} %get-tuple-element.8, f32[]{:T(128)} %get-tuple-element.7, f32[]{:T(128)} %get-tuple-element.6, f32[]{:T(128)S(6)} %sub.29), kind=kLoop, calls=%fused_computation.7 | loop fusion | flops 12730368 | bytes 42434572 | tf_op jit(solution)/shard_map/broadcast_in_dim | solution.py:59
  (33 shorter events, 3.1 us)
Async XLA Ops:
  6.5 3.3 copy-start
  6.5 58.2 %all-gather.7.cloned.1.call-start = ((), (), s32[]{:S(2)}) async-start(), calls=%async_computation | async-start | bytes 4128768 | tf_op jit(solution)/shard_map/all_gather | solution.py:31
  27.5 73.6 %all-gather.9.cloned.1.call-start = ((), (), s32[]{:S(2)}) async-start(), calls=%async_computation.1 | async-start | bytes 4128768 | tf_op jit(solution)/shard_map/all_gather | solution.py:34
  28.6 341.7 %all-gather.11.cloned.1.call-start = ((), (), s32[]{:S(2)}) async-start(), calls=%async_computation.2 | async-start | bytes 66060288 | tf_op jit(solution)/shard_map/all_gather | solution.py:41
  64.8 7.6 copy-start.3
  64.8 15.6 %slice-start = ((s8[8486912]{0:T(1024)(128)(4,1)}), s8[4194304]{0:T(1024)(128)(4,1)S(1)}, s32[]{:S(2)}) async-start(s8[8486912]{0:T(1024)(128)(4,1)} %bitcast.34), calls=%async_computation.4 | async-start | bytes 8388608
  64.8 15.6 %slice-start.1 = ((s8[8486912]{0:T(1024)(128)(4,1)}), s8[4194304]{0:T(1024)(128)(4,1)S(1)}, s32[]{:S(2)}) async-start(s8[8486912]{0:T(1024)(128)(4,1)} %bitcast.34), calls=%async_computation.5 | async-start | bytes 8388608
  72.4 8.0 slice-start.2
  87.7 3.5 copy-start.2
  87.7 664.3 %all-gather.13.cloned.1.call-start = ((), (), s32[]{:S(2)}) async-start(), calls=%async_computation.3 | async-start | bytes 66060288 | tf_op jit(solution)/shard_map/all_gather | solution.py:41
  87.8 304.5 %collective-permute-start = (f32[1184,1792]{1,0:T(8,128)}, f32[1184,1792]{1,0:T(8,128)}, u32[]{:S(2)}, u32[]{:S(2)}) collective-permute-start(f32[1184,1792]{1,0:T(8,128)} %bitcast.32), channel_id=1, source_target_pairs={{0,24},{8,0},{16,8},{24,16},{1,25},{9,1},{17,9},{25,17},{2,26},{10... | collective-permute-start | bytes 25460744 | tf_op jit(solution)/shard_map/ppermute | solution.py:9
  91.1 365.4 %collective-permute-start.1 = (f32[1184,1792]{1,0:T(8,128)}, f32[1184,1792]{1,0:T(8,128)}, u32[]{:S(2)}, u32[]{:S(2)}) collective-permute-start(f32[1184,1792]{1,0:T(8,128)} %bitcast.33), channel_id=1, source_target_pairs={{0,8},{8,16},{16,24},{24,0},{1,9},{9,17},{17,25},{25,1},{2,10},{10... | collective-permute-start | bytes 25460744 | tf_op jit(solution)/shard_map/ppermute | solution.py:9
  486.2 298.4 %collective-permute-start.3 = (f32[1184,1792]{1,0:T(8,128)}, f32[1184,1792]{1,0:T(8,128)}, u32[]{:S(2)}, u32[]{:S(2)}) collective-permute-start(f32[1184,1792]{1,0:T(8,128)} %get-tuple-element.8), channel_id=1, source_target_pairs={{0,8},{8,16},{16,24},{24,0},{1,9},{9,17},{17,25},{25,1},{2,10},{10... | collective-permute-start | bytes 25460744 | tf_op jit(solution)/shard_map/ppermute | solution.py:9
  487.7 365.8 %collective-permute-start.2 = (f32[1184,1792]{1,0:T(8,128)}, f32[1184,1792]{1,0:T(8,128)}, u32[]{:S(2)}, u32[]{:S(2)}) collective-permute-start(f32[1184,1792]{1,0:T(8,128)} %get-tuple-element.8), channel_id=1, source_target_pairs={{0,24},{8,0},{16,8},{24,16},{1,25},{9,1},{17,9},{25,17},{2,26},{10... | collective-permute-start | bytes 25460744 | tf_op jit(solution)/shard_map/ppermute | solution.py:9
  853.5 14.3 %copy-start.1 = (s32[4,1024]{1,0:T(4,128)S(1)}, s32[4,1024]{1,0:T(4,128)}, u32[]{:S(2)}) copy-start(s32[4,1024]{1,0:T(4,128)} %param.15) | copy-start | bytes 49156
Sparse Core Ops, SparseCore 0:
  27.6 37.0 all-gather.6
  66.7 34.3 all-gather.8
  103.0 267.2 all-gather.10
  486.3 265.6 all-gather.12
